TPU v7x, 32 devices: a whole 2x2x4 slice. The times are simulated.
32 devices in a mesh: row: 8 (over y, x, core), col: 4 (over z).
Axes of the slice: x: 2, y: 2, z: 4, core: 2. Of those that a mesh axis runs over, the one named last changes fastest.
Arguments:
- stiff_bb: bfloat16 [96, 3, 128, 384], P(('row', 'col')), may hold values from -6 to 6
- stiff_bi: bfloat16 [96, 384, 3072], P(('row', 'col')), may hold values from -6 to 6
- constraint_modes: bfloat16 [96, 3072, 384], P(('row', 'col')), may hold values from -0.109375 to 0.109375
- interior_mass: float32 [96, 3072], P(('row', 'col')), may hold values from 0.25 to 4
- fixed_modes: bfloat16 [96, 3072, 256], P(('row', 'col')), may hold values from -6 to 6
- mass_bb: bfloat16 [96, 3, 128, 384], P(('row', 'col')), may hold values from -6 to 6
- boundary_map: int32 [96, 3], P(('row', 'col')), may hold values from 0 to 191, as said below
Outputs:
- interface_stiffness: float32 [192, 4, 128, 128], P('row', None, 'col')
- interface_mass: float32 [192, 4, 128, 128], P('row', None, 'col')
- mass_coupling: float32 [96, 256, 384], P(('row', 'col'))
Inputs may be any that keep to these rules, and one draw needn't show every extreme that they name: `boundary_map`: row s holds blocks b, b + a, b + c with 0 < a < c < 4, all three in the range of one owner (block // 24). Rows come in aligned row groups of 12; no owner serves more than 2 rows of one row group, and in every draw one owner serves exactly 2 rows of every row group.
All inputs are finite; a program needn't handle non-finite values.
Results may differ from a plain program's by a relative error of at most 0.0029.
Values sent between devices are 32-bit elements; how exact they have to be, the bound alone decides.
A program may use at most 192 MiB of HBM per device.

v0:
```python
import jax
import jax.numpy as jnp
from jax import lax
from jax.sharding import PartitionSpec as P

BAND = 4
BPO = 24


PAIRS = ((0, 0), (1, 1), (2, 2), (0, 1), (0, 2), (1, 2))


def owner_slots(mapping, slots_each):
    owner = mapping[:, 0] // BPO
    places = jnp.arange(owner.shape[0])
    earlier = (owner[:, None] == owner[None, :]) & (places[:, None] > places[None, :])
    return owner * slots_each + jnp.sum(earlier.astype(jnp.int32), axis=1)


def place_blocks(got_map, received, starting_owner):
    limit = BPO * BAND
    targets = []
    for first, second in PAIRS:
        rows = got_map[:, first]
        local = (rows - starting_owner) * BAND + got_map[:, second] - rows
        targets.append(jnp.where(rows >= 0, local, limit))
    flat = jnp.stack(targets, axis=1).reshape(-1)
    values = received.reshape((flat.shape[0],) + received.shape[2:])
    empty = jnp.zeros((limit,) + received.shape[2:], jnp.float32)
    return empty.at[flat].add(values, mode="drop")


def per_device(
    stiff_bb, stiff_bi, constraint_modes, interior_mass, fixed_modes, mass_bb, boundary_map
):
    owners = lax.axis_size("row")
    lanes = lax.axis_size("col")
    starting_owner = lax.axis_index("row") * BPO
    count = stiff_bi.shape[0]
    order = stiff_bi.shape[1]
    width = order // 3
    rows_per_portion = width // lanes
    slots_each = (count * lanes + owners - 1) // owners
    weighted = (interior_mass[:, :, None] * constraint_modes.astype(jnp.float32)).astype(
        jnp.bfloat16
    )
    red_k = stiff_bb.reshape(count, order, order).astype(jnp.float32) + jnp.einsum(
        "sbi,sic->sbc", stiff_bi, constraint_modes, preferred_element_type=jnp.float32
    )
    red_m = mass_bb.reshape(count, order, order).astype(jnp.float32) + jnp.einsum(
        "sib,sic->sbc", constraint_modes, weighted, preferred_element_type=jnp.float32
    )
    coupling = jnp.einsum("sim,sic->smc", fixed_modes, weighted, preferred_element_type=jnp.float32)
    reduced = jnp.stack([red_k, red_m], axis=1)
    pieces = [
        reduced[:, :, first * width : (first + 1) * width, second * width : (second + 1) * width]
        for first, second in PAIRS
    ]
    packets = jnp.stack(pieces, axis=1).reshape(count, 6, 2, lanes, rows_per_portion, width)
    packets = jnp.moveaxis(packets, 3, 0)
    tiled_map = jnp.broadcast_to(boundary_map[None], (lanes, count, 3))
    grouped, group_map = (
        lax.all_to_all(packets, "col", split_axis=0, concat_axis=1, tiled=True),
        lax.all_to_all(tiled_map, "col", split_axis=0, concat_axis=1, tiled=True),
    )
    grouped = grouped.reshape((lanes * count, 6, 2, rows_per_portion, width))
    group_map = group_map.reshape(lanes * count, 3)
    slot = owner_slots(group_map, slots_each)
    outgoing = (
        jnp.zeros((owners * slots_each, 6, 2, rows_per_portion, width), jnp.float32)
        .at[slot]
        .set(grouped)
    )
    out_map = jnp.full((owners * slots_each, 3), -1, jnp.int32).at[slot].set(group_map)
    received, got_map = (
        lax.all_to_all(outgoing, "row", split_axis=0, concat_axis=0, tiled=True),
        lax.all_to_all(out_map, "row", split_axis=0, concat_axis=0, tiled=True),
    )
    band = place_blocks(got_map, received, starting_owner).reshape(
        BPO, BAND, 2, rows_per_portion, width
    )
    return (band[:, :, 0], band[:, :, 1], coupling)


def solution(mesh):
    placed = (
        P(("row", "col"), None, None, None),
        P(("row", "col"), None, None),
        P(("row", "col"), None, None),
        P(("row", "col"), None),
        P(("row", "col"), None, None),
        P(("row", "col"), None, None, None),
        P(("row", "col"), None),
    )
    return jax.shard_map(
        per_device,
        mesh=mesh,
        in_specs=placed,
        out_specs=(
            P("row", None, "col", None),
            P("row", None, "col", None),
            P(("row", "col"), None, None),
        ),
        check_vma=False,
    )
```

profile of v0, /device:TPU:0, one launch (start us, length us, event | category | flops | bytes accessed | tf_op | source)
XLA Modules:
  0.0 155.5 jit_solution(10635239458374411318)
XLA Ops:
  0.6 0.8 copy.48
  1.4 0.6 broadcast_in_dim.34
  2.0 6.3 %all-to-all-start = ((s32[4,3,3]{1,2,0:T(4,128)}), s32[4,3,3]{1,2,0:T(4,128)S(1)}, u32[]{:S(2)}, u32[]{:S(2)}) async-start(s32[4,3,3]{1,2,0:T(4,128)} %broadcast_in_dim.34), calls=%async_computation | async-start | bytes 16384 | tf_op jit(solution)/shard_map/all_to_all | solution.py:64
  8.3 10.2 %fusion.4 = f32[3,1,384,384]{3,2,0,1:T(8,128)S(1)} fusion(bf16[3,384,384]{2,1,0:T(8,128)(2,1)} %bitcast.65, bf16[3,3072,384]{2,1,0:T(8,128)(2,1)} %param.9, f32[3,3072]{1,0:T(4,128)} %param.10), kind=kOutput, calls=%fused_computation.10 | convolution fusion | flops 2729410560 | bytes 9768960 | tf_op jit(solution)/shard_map/sib,sic->sbc/dot_general | solution.py:50
  18.6 8.2 %fusion.5 = f32[3,1,384,384]{3,2,0,1:T(8,128)S(1)} fusion(bf16[3,384,384]{2,1,0:T(8,128)(2,1)S(1)} %bitcast.66, bf16[3,384,3072]{2,1,0:T(8,128)(2,1)} %param.8, bf16[3,3072,384]{2,1,0:T(8,128)(2,1)} %param.9), kind=kOutput, calls=%fused_computation.12 | convolution fusion | flops 2718793728 | bytes 16809984 | tf_op jit(solution)/shard_map/sbi,sic->sbc/dot_general | solution.py:47
  26.8 0.3 pad_maximum_fusion
  27.3 1.7 %copy.77 = f32[3,6,2,4,32,128]{5,4,2,1,0,3:T(8,128)} copy(f32[3,6,2,4,32,128]{5,4,3,0,2,1:T(8,128)S(1)} %constant_dynamic-update-slice_fusion) | data formatting | bytes 4718592 | tf_op jit(solution)/shard_map/stack | solution.py:59
  29.0 5.1 %all-to-all-start.2 = ((f32[4,3,6,2,32,128]{5,4,3,2,1,0:T(8,128)}), f32[4,3,6,2,32,128]{5,4,3,2,1,0:T(8,128)S(1)}, u32[]{:S(2)}, u32[]{:S(2)}) async-start(f32[4,3,6,2,32,128]{5,4,3,2,1,0:T(8,128)} %bitcast.57), calls=%async_computation.2 | async-start | bytes 4718592 | tf_op jit(solution)/shard_map/all_to_all | solution.py:63
  34.2 0.1 copy.50
  34.3 0.2 convert_reduce_fusion
  34.5 1.2 scatter_custom_fusion
  35.7 51.7 %all-to-all-done.2 = f32[4,3,6,2,32,128]{5,4,3,2,1,0:T(8,128)S(1)} async-done(((f32[4,3,6,2,32,128]{5,4,3,2,1,0:T(8,128)}), f32[4,3,6,2,32,128]{5,4,3,2,1,0:T(8,128)S(1)}, u32[]{:S(2)}, u32[]{:S(2)}) %all-to-all-start.2) | async-done | bytes 2359328 | tf_op jit(solution)/shard_map/all_to_all | solution.py:63
  87.4 3.7 %all-to-all-start.1 = ((s32[8,2,3]{2,1,0:T(2,128)}), s32[8,2,3]{2,1,0:T(2,128)S(1)}, u32[]{:S(2)}, u32[]{:S(2)}) async-start(s32[8,2,3]{2,1,0:T(2,128)} %bitcast.5), calls=%async_computation.1 | async-start | bytes 16384 | tf_op jit(solution)/shard_map/all_to_all | solution.py:77
  91.1 2.0 %broadcast_in_dim.36 = f32[16,6,2,32,128]{4,3,2,1,0:T(8,128)} broadcast(f32[]{:T(128)} %constant.11.clone.1), dimensions={} | broadcast | bytes 3145732 | tf_op jit(solution)/shard_map/broadcast_in_dim | solution.py:70
  93.1 5.8 %scatter_fusion = f32[16,6,2,32,128]{4,3,2,1,0:T(8,128)} fusion(f32[16,6,2,32,128]{4,3,2,1,0:T(8,128)} %broadcast_in_dim.36, s32[12]{0:T(128)S(1)} %fusion.10, f32[12,6,2,32,128]{4,3,2,1,0:T(8,128)S(1)} %bitcast.56), kind=kCustom, calls=%fused_computation.1 | custom fusion | bytes 7077936 | tf_op jit(solution)/shard_map/scatter | solution.py:72
  98.9 4.3 %all-to-all-start.3 = ((f32[16,6,2,32,128]{4,3,2,1,0:T(8,128)}), f32[16,6,2,32,128]{4,3,2,1,0:T(8,128)S(1)}, u32[]{:S(2)}, u32[]{:S(2)}) async-start(f32[16,6,2,32,128]{4,3,2,1,0:T(8,128)} %scatter_fusion), calls=%async_computation.3 | async-start | bytes 6291456 | tf_op jit(solution)/shard_map/all_to_all | solution.py:76
  103.2 9.6 %fusion.6 = f32[3,256,384]{1,2,0:T(8,128)} fusion(bf16[3,3072,256]{2,1,0:T(8,128)(2,1)} %param.11, bf16[3,3072,384]{2,1,0:T(8,128)(2,1)} %param.9, f32[3,3072]{1,0:T(4,128)S(1)} %copy-done.2), kind=kOutput, calls=%fused_computation.15 | convolution fusion | flops 1822556160 | bytes 13012992 | tf_op jit(solution)/shard_map/sim,sic->smc/dot_general | solution.py:53
  112.8 2.7 %copy.65 = f32[3,256,384]{2,1,0:T(8,128)} copy(f32[3,256,384]{1,2,0:T(8,128)} %fusion.6) | data formatting | bytes 2359296
  115.9 0.1 reshape.110
  116.0 25.1 %all-to-all-done.3 = f32[16,6,2,32,128]{4,3,2,1,0:T(8,128)S(1)} async-done(((f32[16,6,2,32,128]{4,3,2,1,0:T(8,128)}), f32[16,6,2,32,128]{4,3,2,1,0:T(8,128)S(1)}, u32[]{:S(2)}, u32[]{:S(2)}) %all-to-all-start.3) | async-done | bytes 3145760 | tf_op jit(solution)/shard_map/all_to_all | solution.py:76
  141.1 1.6 %copy-done = f32[16,6,2,32,128]{4,3,2,1,0:T(8,128)} copy-done((f32[16,6,2,32,128]{4,3,2,1,0:T(8,128)}, f32[16,6,2,32,128]{4,3,2,1,0:T(8,128)S(1)}, u32[]{:S(2)}) %copy-start) | copy-done | bytes 3145752
  142.7 0.4 broadcast_in_dim.32
  143.1 10.3 %scatter_fusion.1 = f32[96,2,32,128]{3,2,1,0:T(8,128)S(1)} fusion(f32[96,2,32,128]{3,2,1,0:T(8,128)S(1)} %broadcast_in_dim.32, s32[96]{0:T(128)S(1)} %fusion.11, f32[96,2,32,128]{3,2,1,0:T(8,128)} %bitcast.55), kind=kCustom, calls=%fused_computation.2 | custom fusion | flops 786432 | bytes 9437568 | tf_op jit(solution)/shard_map/scatter-add | solution.py:30
  153.4 2.1 %slice_bitcast_fusion = (f32[24,4,32,128]{3,2,1,0:T(8,128)}, f32[24,4,32,128]{3,2,1,0:T(8,128)}) fusion(f32[24,4,2,32,128]{4,3,2,1,0:T(8,128)S(1)} %bitcast.54), kind=kLoop, calls=%fused_computation.13 | loop fusion | bytes 6291456 | tf_op jit(solution)/shard_map/squeeze | solution.py:82
  (26 shorter events, 0.8 us)
Async XLA Ops:
  2.0 27.0 %all-to-all-start = ((s32[4,3,3]{1,2,0:T(4,128)}), s32[4,3,3]{1,2,0:T(4,128)S(1)}, u32[]{:S(2)}, u32[]{:S(2)}) async-start(s32[4,3,3]{1,2,0:T(4,128)} %broadcast_in_dim.34), calls=%async_computation | async-start | bytes 16384 | tf_op jit(solution)/shard_map/all_to_all | solution.py:64
  8.3 10.2 %copy-start.1 = (bf16[3,3,128,384]{3,2,1,0:T(8,128)(2,1)S(1)}, bf16[3,3,128,384]{3,2,1,0:T(8,128)(2,1)}, u32[]{:S(2)}) copy-start(bf16[3,3,128,384]{3,2,1,0:T(8,128)(2,1)} %param.7) | copy-start | bytes 2654212
  29.0 58.3 %all-to-all-start.2 = ((f32[4,3,6,2,32,128]{5,4,3,2,1,0:T(8,128)}), f32[4,3,6,2,32,128]{5,4,3,2,1,0:T(8,128)S(1)}, u32[]{:S(2)}, u32[]{:S(2)}) async-start(f32[4,3,6,2,32,128]{5,4,3,2,1,0:T(8,128)} %bitcast.57), calls=%async_computation.2 | async-start | bytes 4718592 | tf_op jit(solution)/shard_map/all_to_all | solution.py:63
  87.4 11.5 %all-to-all-start.1 = ((s32[8,2,3]{2,1,0:T(2,128)}), s32[8,2,3]{2,1,0:T(2,128)S(1)}, u32[]{:S(2)}, u32[]{:S(2)}) async-start(s32[8,2,3]{2,1,0:T(2,128)} %bitcast.5), calls=%async_computation.1 | async-start | bytes 16384 | tf_op jit(solution)/shard_map/all_to_all | solution.py:77
  98.9 4.3 %copy-start.2 = (f32[3,3072]{1,0:T(4,128)S(1)}, f32[3,3072]{1,0:T(4,128)}, u32[]{:S(2)}) copy-start(f32[3,3072]{1,0:T(4,128)} %param.10) | copy-start | bytes 110596
  98.9 42.2 %all-to-all-start.3 = ((f32[16,6,2,32,128]{4,3,2,1,0:T(8,128)}), f32[16,6,2,32,128]{4,3,2,1,0:T(8,128)S(1)}, u32[]{:S(2)}, u32[]{:S(2)}) async-start(f32[16,6,2,32,128]{4,3,2,1,0:T(8,128)} %scatter_fusion), calls=%async_computation.3 | async-start | bytes 6291456 | tf_op jit(solution)/shard_map/all_to_all | solution.py:76
  141.1 1.7 %copy-start = (f32[16,6,2,32,128]{4,3,2,1,0:T(8,128)}, f32[16,6,2,32,128]{4,3,2,1,0:T(8,128)S(1)}, u32[]{:S(2)}) copy-start(f32[16,6,2,32,128]{4,3,2,1,0:T(8,128)S(1)} %all-to-all-done.3) | copy-start | bytes 9437188
where the time goes:
time: 156 us
  waiting for transfers between devices  76.8 us (49%)
  matrix products  28 us (18%)
  local copies, waits for them, and re-layouts  19.7 us (13%)
  starting transfers between devices  19.5 us (12%)
  other arithmetic  10.8 us (7%)
    all_to_all x1, waiting for transfers between devices, per_device(): lax.all_to_all(packets, 'col', split_axis=0, concat_axis=1, tiled=True)  51.7 us
    all_to_all x1, waiting for transfers between devices, per_device(): lax.all_to_all(outgoing, 'row', split_axis=0, concat_axis=0, tiled=True)  25.1 us
    scatter-add x1, other arithmetic, place_blocks(): return empty.at[flat].add(values, mode='drop')  10.3 us
    dot_general x1, matrix products, per_device(): jnp.einsum('sib,sic->sbc', constraint_modes, weighted, preferred_element_...  10.2 us
    dot_general x1, matrix products, per_device(): jnp.einsum('sim,sic->smc', fixed_modes, weighted, preferred_element_type=...  9.56 us
    dot_general x1, matrix products, per_device(): jnp.einsum('sbi,sic->sbc', stiff_bi, constraint_modes, preferred_element_...  8.2 us
    all_to_all x1, starting transfers between devices, per_device(): lax.all_to_all(tiled_map, 'col', split_axis=0, concat_axis=1, tiled=True)  6.35 us
    scatter x1, local copies, waits for them, and re-layouts, per_device(): outgoing = jnp.zeros((owners * slots_each, 6, 2, rows_per_portion, width)...  5.76 us
  transfers between devices with their start and end apart: 4, of which 2 were waited for; matrix products, arithmetic and copies ran while one was open for 27% of the time, Pallas kernels for 0%

commit v1 on v0

v1 whole, which is shorter than its diff:
```python
import functools
import jax
import jax.numpy as jnp
from jax import lax
from jax.experimental import pallas as pl
from jax.experimental.pallas import tpu as pltpu
from jax.sharding import PartitionSpec as P

BAND = 4
BPO = 24
LANE = 128

PAIRS = ((0, 0), (1, 1), (2, 2), (0, 1), (0, 2), (1, 2))
KINDS = 2
CHUNKS = KINDS * len(PAIRS)
MESH = pl.DeviceIdType.MESH
VMEM_LIMIT = 60 * 1024 * 1024


def at_col(z):
    return {"row": lax.axis_index("row"), "col": z}


def at_row(r):
    return {"row": r, "col": lax.axis_index("col")}


def reduce_and_send(
    owners, lanes, slots,
    kbb, kbi, psi, mass, modes, mbb, table,
    got, all_maps, coupling,
    kbb_v, kbi_v, psi_v, modes_v, mbb_v, weighted, coupled, product,
    reduced, grouped, staging, outgoing, maps_v, maps_s,
    in_sems, z_send, z_recv, r_send, r_recv, r_own,
    zm_send, zm_recv, rm_send, rm_recv, small, out_sems,
):
    count, order, inner = kbi.shape
    width = order // 3
    part = width // lanes
    members = count * lanes
    row = lax.axis_index("row")
    col = lax.axis_index("col")

    def loads(s):
        return (
            pltpu.make_async_copy(kbi.at[s], kbi_v.at[s], in_sems.at[0, s]),
            pltpu.make_async_copy(psi.at[s], psi_v.at[s], in_sems.at[1, s]),
            pltpu.make_async_copy(kbb.at[s], kbb_v.at[s], in_sems.at[2, s]),
        )

    def late_loads(s):
        return (
            pltpu.make_async_copy(mbb.at[s], mbb_v.at[s], in_sems.at[3, s]),
            pltpu.make_async_copy(modes.at[s], modes_v.at[s], in_sems.at[4, s]),
        )

    for s in range(count):
        for copy in loads(s):
            copy.start()
    for s in range(count):
        for copy in late_loads(s):
            copy.start()

    barrier = pltpu.get_barrier_semaphore()
    for i in range(1, lanes):
        pl.semaphore_signal(barrier, inc=1, device_id=at_col(lax.rem(col + i, lanes)), device_id_type=MESH)

    def greet(i, carry):
        pl.semaphore_signal(barrier, inc=1, device_id=at_row(lax.rem(row + i, owners)), device_id_type=MESH)
        return carry

    lax.fori_loop(1, owners, greet, 0)

    def put(kind, s, total):
        for p, (i, j) in enumerate(PAIRS):
            block = total[i * width : (i + 1) * width, j * width : (j + 1) * width]
            reduced[kind * len(PAIRS) + p, :, s] = block.reshape(lanes, part, width)

    def stiffness(s, carry):
        for copy in loads(s):
            copy.wait()
        product[...] = jnp.dot(kbi_v[s], psi_v[s], preferred_element_type=jnp.float32)
        put(0, s, product[...] + kbb_v[s].astype(jnp.float32).reshape(order, order))
        return carry

    lax.fori_loop(0, count, stiffness, 0)
    pl.semaphore_wait(barrier, lanes - 1 + owners - 1)

    def z_map(i):
        return pltpu.make_async_remote_copy(
            src_ref=table, dst_ref=maps_v.at[col],
            send_sem=zm_send.at[i], recv_sem=zm_recv.at[lanes - i],
            device_id=at_col(lax.rem(col + i, lanes)), device_id_type=MESH,
        )

    def z_copy(p, i):
        to = lax.rem(col + i, lanes)
        return pltpu.make_async_remote_copy(
            src_ref=reduced.at[p, to], dst_ref=grouped.at[p, col],
            send_sem=z_send.at[p, i], recv_sem=z_recv.at[p, lanes - i],
            device_id=at_col(to), device_id_type=MESH,
        )

    for i in range(1, lanes):
        z_map(i).start()
    maps_v[col] = table[...]

    half = len(PAIRS)

    def send_chunk(p, carry):
        for i in range(1, lanes):
            z_copy(p, i).start()
        grouped[p, col] = reduced[p, col]
        return carry

    lax.fori_loop(0, half, send_chunk, 0)

    def masses(s, carry):
        for copy in late_loads(s):
            copy.wait()

        def weigh(k, inner_carry):
            start = pl.multiple_of(k * LANE, LANE)
            lines = mass[:, pl.ds(start, LANE)]
            chosen = lax.broadcasted_iota(jnp.int32, lines.shape, 0) == s
            line = jnp.sum(jnp.where(chosen, lines, 0.0), axis=0, keepdims=True)
            column = jnp.broadcast_to(line, (LANE, LANE)).T
            scale = jnp.concatenate([column] * (order // LANE), axis=1)
            values = psi_v[s, pl.ds(start, LANE), :].astype(jnp.float32)
            weighted[pl.ds(start, LANE), :] = (scale * values).astype(jnp.bfloat16)
            return inner_carry

        lax.fori_loop(0, inner // LANE, weigh, 0)
        across = (((0,), (0,)), ((), ()))
        product[...] = lax.dot_general(psi_v[s], weighted[...], across, preferred_element_type=jnp.float32)
        put(1, s, product[...] + mbb_v[s].astype(jnp.float32).reshape(order, order))
        coupled[s] = lax.dot_general(modes_v[s], weighted[...], across, preferred_element_type=jnp.float32)
        pltpu.make_async_copy(coupled.at[s], coupling.at[s], out_sems.at[s]).start()
        return carry

    lax.fori_loop(0, count, masses, 0)
    lax.fori_loop(half, CHUNKS, send_chunk, 0)

    for i in range(1, lanes):
        z_map(i).wait()
    to_scalar = pltpu.make_async_copy(maps_v, maps_s, small.at[0])
    to_scalar.start()

    def r_map(i):
        return pltpu.make_async_remote_copy(
            src_ref=maps_v, dst_ref=all_maps.at[row],
            send_sem=rm_send.at[i], recv_sem=rm_recv.at[owners - i],
            device_id=at_row(lax.rem(row + i, owners)), device_id_type=MESH,
        )

    lax.fori_loop(1, owners, lambda i, c: (r_map(i).start(), c)[1], 0)
    own_map = pltpu.make_async_copy(maps_v, all_maps.at[row], small.at[1])
    own_map.start()
    to_scalar.wait()

    belongs = [maps_s[m // count, 0, 3 * (m % count)] // BPO for m in range(members)]
    ranks = []
    for m in range(members):
        rank = jnp.int32(0)
        for e in range(m):
            rank = rank + jnp.where(belongs[e] == belongs[m], 1, 0)
        ranks.append(rank)
    places = [belongs[m] * slots + ranks[m] for m in range(members)]

    chosen = []
    for slot in range(owners * slots):
        member = jnp.int32(0)
        for m in range(1, members):
            member = jnp.where(places[m] == slot, m, member)
        chosen.append(member)

    def forward(p, carry):
        for i in range(1, lanes):
            z_copy(p, i).wait_recv()

        staging[...] = grouped[p].reshape(members, part, width)
        for slot, member in enumerate(chosen):
            outgoing[p, slot // slots, slot % slots] = staging[member]

        def ship(i, inner_carry):
            r_copy(p, i).start()
            return inner_carry

        lax.fori_loop(1, owners, ship, 0)
        own_copy(p).start()
        return carry

    def r_copy(p, i):
        to = lax.rem(row + i, owners)
        return pltpu.make_async_remote_copy(
            src_ref=outgoing.at[p, to], dst_ref=got.at[p, row],
            send_sem=r_send.at[p], recv_sem=r_recv.at[p],
            device_id=at_row(to), device_id_type=MESH,
        )

    def own_copy(p):
        return pltpu.make_async_copy(outgoing.at[p, row], got.at[p, row], r_own.at[p])

    lax.fori_loop(0, CHUNKS, forward, 0)

    def settle(p, carry):
        for i in range(1, lanes):
            z_copy(p, i).wait_send()
        rest = got.at[p, pl.ds(0, owners - 1)]
        pltpu.make_async_copy(rest, rest, r_send.at[p]).wait()
        pltpu.make_async_copy(rest, rest, r_recv.at[p]).wait()
        own_copy(p).wait()
        return carry

    lax.fori_loop(0, CHUNKS, settle, 0)
    lax.fori_loop(1, owners, lambda i, c: (r_map(i).wait(), c)[1], 0)
    own_map.wait()
    for s in range(count):
        pltpu.make_async_copy(coupled.at[s], coupling.at[s], out_sems.at[s]).wait()


def assemble(owners, lanes, count, slots, got, all_maps, k_out, m_out, buffer, maps_s, sems, small):
    to_scalar = pltpu.make_async_copy(all_maps.at[:, :, pl.ds(0, 1)], maps_s, small.at[0])
    to_scalar.start()
    for p in range(CHUNKS):
        pltpu.make_async_copy(got.at[p], buffer.at[p], sems.at[p]).start()
    k_out[...] = jnp.zeros_like(k_out)
    m_out[...] = jnp.zeros_like(m_out)
    to_scalar.wait()
    for p in range(CHUNKS):
        pltpu.make_async_copy(got.at[p], buffer.at[p], sems.at[p]).wait()
    me = lax.axis_index("row")
    first = me * BPO

    def per_group(group, carry):
        def per_member(m, filled):
            z, s = m // count, m % count
            blocks = [maps_s[group, z, 0, 3 * s + k] for k in range(3)]
            mine = blocks[0] // BPO == me

            @pl.when(mine)
            def _():
                for p, (i, j) in enumerate(PAIRS):
                    at, offset = blocks[i] - first, blocks[j] - blocks[i]
                    k_out[at, offset] += buffer[p, group, filled]
                    m_out[at, offset] += buffer[len(PAIRS) + p, group, filled]

            return filled + jnp.where(mine, 1, 0)

        lax.fori_loop(0, count * lanes, per_member, jnp.int32(0))
        return carry

    lax.fori_loop(0, owners, per_group, 0)


def per_device(
    stiff_bb, stiff_bi, constraint_modes, interior_mass, fixed_modes, mass_bb, boundary_map
):
    owners = lax.axis_size("row")
    lanes = lax.axis_size("col")
    count, order, inner = stiff_bi.shape
    modes = fixed_modes.shape[2]
    width = order // 3
    part = width // lanes
    slots = (count * lanes + owners - 1) // owners
    f32, bf16 = jnp.float32, jnp.bfloat16
    table = jnp.pad(boundary_map.reshape(1, count * 3), ((0, 7), (0, LANE - count * 3)))
    hbm = pl.BlockSpec(memory_space=pl.ANY)
    vmem = pl.BlockSpec(memory_space=pltpu.VMEM)
    dma = pltpu.SemaphoreType.DMA
    got, all_maps, coupling = pl.pallas_call(
        functools.partial(reduce_and_send, owners, lanes, slots),
        out_shape=(
            jax.ShapeDtypeStruct((CHUNKS, owners, slots, part, width), f32),
            jax.ShapeDtypeStruct((owners, lanes, 8, LANE), jnp.int32),
            jax.ShapeDtypeStruct((count, modes, order), f32),
        ),
        in_specs=[hbm, hbm, hbm, vmem, hbm, hbm, vmem],
        out_specs=(hbm, hbm, hbm),
        scratch_shapes=[
            pltpu.VMEM((count, 3, width, order), bf16),
            pltpu.VMEM((count, order, inner), bf16),
            pltpu.VMEM((count, inner, order), bf16),
            pltpu.VMEM((count, inner, modes), bf16),
            pltpu.VMEM((count, 3, width, order), bf16),
            pltpu.VMEM((inner, order), bf16),
            pltpu.VMEM((count, modes, order), f32),
            pltpu.VMEM((order, order), f32),
            pltpu.VMEM((CHUNKS, lanes, count, part, width), f32),
            pltpu.VMEM((CHUNKS, lanes, count, part, width), f32),
            pltpu.VMEM((lanes * count, part, width), f32),
            pltpu.VMEM((CHUNKS, owners, slots, part, width), f32),
            pltpu.VMEM((lanes, 8, LANE), jnp.int32),
            pltpu.SMEM((lanes, 8, LANE), jnp.int32),
            dma((5, count)),
            dma((CHUNKS, lanes)),
            dma((CHUNKS, lanes)),
            dma((CHUNKS,)),
            dma((CHUNKS,)),
            dma((CHUNKS,)),
            dma((lanes,)),
            dma((lanes,)),
            dma((owners,)),
            dma((owners,)),
            dma((2,)),
            dma((count,)),
        ],
        compiler_params=pltpu.CompilerParams(
            collective_id=0, has_side_effects=True, vmem_limit_bytes=VMEM_LIMIT
        ),
        name="reduce_and_send",
    )(stiff_bb, stiff_bi, constraint_modes, interior_mass, fixed_modes, mass_bb, table)
    block = jax.ShapeDtypeStruct((BPO, BAND, part, width), f32)
    k_out, m_out = pl.pallas_call(
        functools.partial(assemble, owners, lanes, count, slots),
        out_shape=(block, block),
        in_specs=[hbm, hbm],
        out_specs=(vmem, vmem),
        scratch_shapes=[
            pltpu.VMEM(got.shape, f32),
            pltpu.SMEM((owners, lanes, 1, LANE), jnp.int32),
            dma((CHUNKS,)),
            dma((1,)),
        ],
        compiler_params=pltpu.CompilerParams(vmem_limit_bytes=VMEM_LIMIT),
        name="assemble",
    )(got, all_maps)
    return k_out, m_out, coupling


def solution(mesh):
    placed = (
        P(("row", "col"), None, None, None),
        P(("row", "col"), None, None),
        P(("row", "col"), None, None),
        P(("row", "col"), None),
        P(("row", "col"), None, None),
        P(("row", "col"), None, None, None),
        P(("row", "col"), None),
    )
    return jax.shard_map(
        per_device,
        mesh=mesh,
        in_specs=placed,
        out_specs=(
            P("row", None, "col", None),
            P("row", None, "col", None),
            P(("row", "col"), None, None),
        ),
        check_vma=False,
    )
```

time: 156 us -> 83 us (0.53)
  Pallas kernels: 0 us -> 79.6 us
  waiting for transfers between devices: 76.8 us -> 0 us
  matrix products: 28 us -> 0 us
  starting transfers between devices: 19.5 us -> 0 us
  local copies, waits for them, and re-layouts: 19.7 us -> 2.38 us
  other arithmetic: 10.8 us -> 0 us
    pallas_call x0 -> x2, Pallas kernels: none -> 79.6 us  [the longest x1 72.3 us: per_device(): pl.pallas_call(functools.partial(reduce_and_send, owners, lanes, slots),...]
    all_to_all x4 -> x0, waiting for transfers between devices: 76.8 us -> none  [the longest x1 51.7 us: per_device(): lax.all_to_all(packets, 'col', split_axis=0, concat_axis=1, tiled=True)]
    dot_general x3 -> x0, matrix products: 28 us -> none  [the longest x1 10.2 us: per_device(): jnp.einsum('sib,sic->sbc', constraint_modes, weighted, preferred_element_...]
    all_to_all x4 -> x0, starting transfers between devices: 19.5 us -> none  [the longest x1 6.35 us: per_device(): lax.all_to_all(tiled_map, 'col', split_axis=0, concat_axis=1, tiled=True)]
    scatter-add x1 -> x0, other arithmetic: 10.3 us -> none  [place_blocks(): return empty.at[flat].add(values, mode='drop')]
    scatter x2 -> x0, local copies, waits for them, and re-layouts: 6.94 us -> none  [the longest x1 5.76 us: per_device(): outgoing = jnp.zeros((owners * slots_each, 6, 2, rows_per_portion, width)...]
    unnamed x16 -> x3, local copies, waits for them, and re-layouts: 5.47 us -> 1.02 us
    broadcast_in_dim x3 -> x0, local copies, waits for them, and re-layouts: 3.03 us -> none  [the longest x1 2.05 us: per_device(): jnp.zeros((owners * slots_each, 6, 2, rows_per_portion, width), jnp.float32)]
  transfers between devices with their start and end apart: 4 -> 0, of which waited for: 2 -> 0; matrix products, arithmetic and copies ran while one was open for 27% -> 0% of each run, Pallas kernels for 0% -> 0%
where the time goes in v1:
time: 83 us; the launch traced here: 82.7 us
  Pallas kernels  79.6 us (96%)
  local copies, waits for them, and re-layouts  2.38 us (3%)
    pallas_call x1, Pallas kernels, per_device(): pl.pallas_call(functools.partial(reduce_and_send, owners, lanes, slots),...  72.3 us
    pallas_call x1, Pallas kernels, per_device(): pl.pallas_call(functools.partial(assemble, owners, lanes, count, slots),...  7.38 us

profile of v1, /device:TPU:0, one launch (start us, length us, event | category | flops | bytes accessed | tf_op | source)
XLA Modules:
  0.0 82.7 jit_solution(2733723442550894367)
XLA Ops:
  0.6 0.8 reshape.9
  1.4 0.6 pad.4.table
  2.0 72.3 %reduce_and_send.1 = (f32[12,8,2,32,128]{4,3,2,1,0:T(8,128)}, s32[8,4,8,128]{3,2,1,0:T(8,128)}, f32[3,256,384]{2,1,0:T(8,128)}) custom-call(bf16[3,3,128,384]{3,2,1,0:T(8,128)(2,1)} %kbb.1, bf16[3,384,3072]{2,1,0:T(8,128)(2,1)} %kbi.1, bf16[3,3072,384]{2,1,0:T(8,128)(2,1)} %psi.1, f32[3,3072]{1,0:T(4,128)} %mass.1, bf16[3,3072,256]{2,1,0:T(8,128)(2,1)} %modes.1, ...), custom_call_target="tpu_custom_call" | custom-call | tf_op jit(solution)/shard_map/reduce_and_send/pallas_call | solution.py:271
  74.3 0.0 copy-start
  74.3 7.4 %assemble.1 = (f32[24,4,32,128]{3,2,1,0:T(8,128)}, f32[24,4,32,128]{3,2,1,0:T(8,128)}) custom-call(f32[12,8,2,32,128]{4,3,2,1,0:T(8,128)} %get-tuple-element.8.got, s32[8,4,8,128]{3,2,1,0:T(8,128)} %get-tuple-element.9.all_maps), custom_call_target="tpu_custom_call" | custom-call | tf_op jit(solution)/shard_map/assemble/pallas_call | solution.py:314
  81.7 0.0 copy-done
  81.7 1.0 %copy.11 = f32[3,256,384]{2,1,0:T(8,128)} copy(f32[3,256,384]{2,1,0:T(8,128)S(1)} %copy-done) | data formatting | bytes 2359296
Async XLA Ops:
  74.3 7.4 %copy-start = (f32[3,256,384]{2,1,0:T(8,128)S(1)}, f32[3,256,384]{2,1,0:T(8,128)}, u32[]{:S(2)}) copy-start(f32[3,256,384]{2,1,0:T(8,128)} %get-tuple-element.18) | copy-start | bytes 3538948
